TPU v7x, 32 devices: a whole 2x2x4 slice. The times are simulated.
32 devices in a mesh: tm: 16 (over z, y, core), asset: 2 (over x).
Axes of the slice: x: 2, y: 2, z: 4, core: 2. Of those that a mesh axis runs over, the one named last changes fastest.
Arguments:
- returns: bfloat16 [64, 8192], P('tm', 'asset'), as said below
- signal: bfloat16 [64, 8192], P('tm', 'asset'), may hold values from -6 to 6
- earlier: bfloat16 [59, 8192], P(None, 'asset'), as said below
Outputs:
- filtered: float32 [64, 8192], P('tm', 'asset')
Inputs may be any that keep to these rules, and one draw needn't show every extreme that they name: Each equity has its own scale of returns, the same in returns and earlier. `earlier`: drawn by the same law as returns, with the same scale for each equity.
All inputs are finite; a program needn't handle non-finite values.
Results may differ from a plain program's by a relative error of at most 0.0032.
Values may be sent and summed in bfloat16 or wider, within the bound.
No kernel may reach another device: no remote copies, remote signals or barrier semaphores. Data moves between devices by JAX's collectives and lax.ppermute only.
A program may use at most 64 MiB of HBM per device.

v0:
```python
import jax
import jax.numpy as jnp
from jax import lax
from jax.sharding import PartitionSpec as P

WIN = 60
HIST = 59


var_floor = 0.05
shrink_level = 0.1


def moments(window):
    values = window.astype(jnp.float32)
    center = jnp.mean(values, axis=0)
    spread = jnp.mean(values * values, axis=0) - center * center
    return (center, jnp.sqrt(jnp.maximum(spread, var_floor)))


def contribution(ext_rows, ext_cols, signal_cols):

    def one_day(day_index):
        window_rows = lax.dynamic_slice_in_dim(ext_rows, day_index, WIN, 0)
        window_cols = lax.dynamic_slice_in_dim(ext_cols, day_index, WIN, 0)
        mean_rows, scale_rows = moments(window_rows)
        mean_cols, scale_cols = moments(window_cols)
        gram_tile = lax.dot_general(
            window_rows, window_cols, (((0,), (0,)), ((), ())), preferred_element_type=jnp.float32
        )
        correlation = (gram_tile / WIN - mean_rows[:, None] * mean_cols[None, :]) / (
            scale_rows[:, None] * scale_cols[None, :]
        )
        shrunk = (
            jnp.sign(correlation) * jnp.maximum(jnp.abs(correlation) - shrink_level, 0.0)
        ).astype(jnp.bfloat16)
        day_signal = lax.dynamic_index_in_dim(signal_cols, day_index, 0, keepdims=False)
        return jnp.dot(shrunk, day_signal, preferred_element_type=jnp.float32)

    return lax.map(one_day, jnp.arange(signal_cols.shape[0], dtype=jnp.int32))


def history(block_rows, earlier_rows):
    day_dev = block_rows.shape[0]
    position = lax.axis_index("tm")
    span = HIST + day_dev
    all_days = lax.all_gather(block_rows, "tm", axis=0, tiled=True)
    sequence = jnp.concatenate([earlier_rows, all_days], 0)
    return lax.dynamic_slice_in_dim(sequence, position * day_dev, span, 0)


def per_device(returns, signal, earlier):
    extended = history(returns, earlier)
    return contribution(
        extended,
        lax.all_gather(extended, "asset", axis=1, tiled=True),
        lax.all_gather(signal, "asset", axis=1, tiled=True),
    )


def solution(mesh):
    in_specs = (P("tm", "asset"), P("tm", "asset"), P(None, "asset"))
    out_specs = P("tm", "asset")
    return jax.shard_map(
        per_device, mesh=mesh, in_specs=in_specs, out_specs=out_specs, check_vma=False
    )
```

profile of v0, /device:TPU:0, one launch (start us, length us, event | category | flops | bytes accessed | tf_op | source)
XLA Modules:
  0.0 396.4 jit_solution(13054484988312092439)
XLA Ops:
  0.0 0.0 copy-start
  0.0 24.9 %all-gather = bf16[16,4,4096]{2,1,0:T(4,128)(2,1)S(1)} all-gather(bf16[1,4,4096]{2,1,0:T(4,128)(2,1)} %bitcast.17), channel_id=1, replica_groups=mesh['tm'=16,'asset'=2] {'tm'}, dimensions={0}, use_global_device_ids=true | all-gather | bytes 557056 | tf_op jit(solution)/shard_map/all_gather | solution.py:47
  24.9 0.1 reshape.31
  25.1 0.0 copy-done
  25.1 0.4 fusion.14
  25.5 0.0 copy-start.1
  25.5 14.8 %all_gather.10 = bf16[63,8192]{1,0:T(8,128)(2,1)S(1)} all-gather(bf16[63,4096]{1,0:T(8,128)(2,1)S(1)} %fusion.14), channel_id=1, replica_groups=mesh['tm'=16,'asset'=2] {'asset'}, dimensions={1}, use_global_device_ids=true | all-gather | bytes 1548288 | tf_op jit(solution)/shard_map/all_gather | solution.py:56
  40.4 0.0 copy-done.1
  40.4 4.7 %all_gather.11 = bf16[4,8192]{1,0:T(4,128)(2,1)} all-gather(bf16[4,4096]{1,0:T(4,128)(2,1)S(1)} %copy-done.1), channel_id=1, replica_groups=mesh['tm'=16,'asset'=2] {'asset'}, dimensions={1}, use_global_device_ids=true | all-gather | bytes 98304 | tf_op jit(solution)/shard_map/all_gather | solution.py:57
  45.1 0.5 iota.3
  45.6 350.8 %while.12 = (s32[]{:T(128)}, f32[4,4096]{1,0:T(4,128)}, s32[4]{0:T(128)}, bf16[63,4096]{1,0:T(8,128)(2,1)S(1)}, bf16[63,8192]{1,0:T(8,128)(2,1)S(1)}, /*index=5*...) while((s32[]{:T(128)}, f32[4,4096]{1,0:T(4,128)}, s32[4]{0:T(128)}, ...), condition=%wide.region_5.6_spmd, body=%wide.region_0.5_spmd.sunk | while | flops 4465725440 | bytes 3515580 | solution.py:40
  45.6 1.2 dynamic_slice.73
  48.7 0.5 convert_reduce_fusion.4
  49.3 0.3 convert_reduce_fusion.5
  50.8 0.9 fusion.34
  51.7 80.1 %fusion.35 = f32[1,4096]{1,0:T(1,128)S(1)} fusion(f32[8192]{0:T(1024)S(1)} %get-tuple-element.150, f32[4096]{0:T(1024)S(1)} %get-tuple-element.153, f32[8192]{0:T(1024)S(1)} %get-tuple-element.154, f32[4096]{0:T(1024)S(1)} %get-tuple-element.155, bf16[63,8192]{1,0:T(8,128)(2,1)S(1)} %get-tuple-element.180, s32[]{:T(128)S(6)} %select_n.20, ...), kind=kOutput, calls=%fused_computation.1.clone.3 | convolution fusion | flops 4462739456 | bytes 1680384 | tf_op jit(solution)/shard_map/while/body/eval_jaxpr/dot_general | solution.py:38
  131.8 1.5 dynamic_update_slice.8
  133.3 1.2 dynamic_slice.73
  136.4 0.5 convert_reduce_fusion.4
  137.0 0.3 convert_reduce_fusion.5
  138.5 0.9 fusion.34
  139.4 80.1 %fusion.35 = f32[1,4096]{1,0:T(1,128)S(1)} fusion(f32[8192]{0:T(1024)S(1)} %get-tuple-element.150, f32[4096]{0:T(1024)S(1)} %get-tuple-element.153, f32[8192]{0:T(1024)S(1)} %get-tuple-element.154, f32[4096]{0:T(1024)S(1)} %get-tuple-element.155, bf16[63,8192]{1,0:T(8,128)(2,1)S(1)} %get-tuple-element.180, s32[]{:T(128)S(6)} %select_n.20, ...), kind=kOutput, calls=%fused_computation.1.clone.3 | convolution fusion | flops 4462739456 | bytes 1680384 | tf_op jit(solution)/shard_map/while/body/eval_jaxpr/dot_general | solution.py:38
  219.5 1.5 dynamic_update_slice.8
  221.0 1.2 dynamic_slice.73
  224.1 0.5 convert_reduce_fusion.4
  224.7 0.3 convert_reduce_fusion.5
  226.2 0.9 fusion.34
  227.1 80.1 %fusion.35 = f32[1,4096]{1,0:T(1,128)S(1)} fusion(f32[8192]{0:T(1024)S(1)} %get-tuple-element.150, f32[4096]{0:T(1024)S(1)} %get-tuple-element.153, f32[8192]{0:T(1024)S(1)} %get-tuple-element.154, f32[4096]{0:T(1024)S(1)} %get-tuple-element.155, bf16[63,8192]{1,0:T(8,128)(2,1)S(1)} %get-tuple-element.180, s32[]{:T(128)S(6)} %select_n.20, ...), kind=kOutput, calls=%fused_computation.1.clone.3 | convolution fusion | flops 4462739456 | bytes 1680384 | tf_op jit(solution)/shard_map/while/body/eval_jaxpr/dot_general | solution.py:38
  307.2 1.5 dynamic_update_slice.8
  308.7 1.2 dynamic_slice.73
  311.8 0.5 convert_reduce_fusion.4
  312.4 0.3 convert_reduce_fusion.5
  313.9 0.9 fusion.34
  314.8 80.1 %fusion.35 = f32[1,4096]{1,0:T(1,128)S(1)} fusion(f32[8192]{0:T(1024)S(1)} %get-tuple-element.150, f32[4096]{0:T(1024)S(1)} %get-tuple-element.153, f32[8192]{0:T(1024)S(1)} %get-tuple-element.154, f32[4096]{0:T(1024)S(1)} %get-tuple-element.155, bf16[63,8192]{1,0:T(8,128)(2,1)S(1)} %get-tuple-element.180, s32[]{:T(128)S(6)} %select_n.20, ...), kind=kOutput, calls=%fused_computation.1.clone.3 | convolution fusion | flops 4462739456 | bytes 1680384 | tf_op jit(solution)/shard_map/while/body/eval_jaxpr/dot_general | solution.py:38
  394.9 1.5 dynamic_update_slice.8
  (9 shorter events, 0.1 us)
Async XLA Ops:
  0.0 25.1 %copy-start = (bf16[59,4096]{1,0:T(8,128)(2,1)S(1)}, bf16[59,4096]{1,0:T(8,128)(2,1)}, u32[]{:S(2)}) copy-start(bf16[59,4096]{1,0:T(8,128)(2,1)} %param.7) | copy-start | bytes 1449988
  25.5 14.9 %copy-start.1 = (bf16[4,4096]{1,0:T(4,128)(2,1)S(1)}, bf16[4,4096]{1,0:T(4,128)(2,1)}, u32[]{:S(2)}) copy-start(bf16[4,4096]{1,0:T(4,128)(2,1)} %param.6) | copy-start | bytes 98308
where the time goes:
time: 397 us; the launch traced here: 396 us
  matrix products  320 us (81%)
  blocking collectives  44.5 us (11%)
  local copies, waits for them, and re-layouts  15.3 us (4%)
  loops' own time  12.5 us (3%)
    dot_general x4, matrix products, one_day(): return jnp.dot(shrunk, day_signal, preferred_element_type=jnp.float32)  320 us
    all_gather x1, blocking collectives, history(): all_days = lax.all_gather(block_rows, 'tm', axis=0, tiled=True)  24.9 us
    all_gather x1, blocking collectives, per_device(): lax.all_gather(extended, 'asset', axis=1, tiled=True)  14.8 us
    another operation x1, loops' own time, contribution(): return lax.map(one_day, jnp.arange(signal_cols.shape[0], dtype=jnp.int32))  12.5 us

commit v1 on v0

v1 whole, which is shorter than its diff:
```python
import functools

import jax
import jax.numpy as jnp
from jax import lax
from jax.experimental import pallas as pl
from jax.experimental.pallas import tpu as pltpu
from jax.sharding import PartitionSpec as P

WIN = 60
HIST = 59
SEG = 64
BLK = 512
CHUNK = 32
VAR_FLOOR = 0.05
SHRINK = 0.1
TINY = 1e-30


def history(block_rows, earlier_rows):
    day_dev = block_rows.shape[0]
    position = lax.axis_index("tm")
    span = HIST + day_dev
    all_days = lax.all_gather(block_rows, "tm", axis=0, tiled=True)
    sequence = jnp.concatenate([earlier_rows, all_days], 0)
    return lax.dynamic_slice_in_dim(sequence, position * day_dev, span, 0)


def pair_kernel(tasks, chunks, it_ref, jt_ref, rt_ref, lhs_ref, rhs_ref, sb_ref, b_ref, racc_ref, cacc_ref):
    def body(accs0, accs1):
        racc_ref[...] = jnp.zeros_like(racc_ref)
        cacc_ref[...] = jnp.zeros_like(cacc_ref)

        @pl.when(pl.program_id(0) == 0)
        def _():
            for c in range(chunks):
                pltpu.matmul_pop(accs0[c])
                pltpu.matmul_pop(accs1[c])

        def trip(t, carry):
            now = jnp.minimum(t, tasks - 1)
            i_now = pl.multiple_of(it_ref[now] * BLK, BLK)
            j_now = pl.multiple_of(jt_ref[now] * BLK, BLK)
            old = jnp.maximum(t - 1, 0)
            i_old = pl.multiple_of(it_ref[old] * BLK, BLK)
            j_old = pl.multiple_of(jt_ref[old] * BLK, BLK)
            r_old = pl.multiple_of(rt_ref[old] * BLK, BLK)
            half = BLK // 2
            pltpu.matmul_push_rhs(rhs_ref[0, :, pl.ds(i_now, half)], staging_register=0, mxu_index=0)
            pltpu.matmul_push_rhs(rhs_ref[0, :, pl.ds(i_now + half, half)], staging_register=0, mxu_index=1)
            bound = [b_ref[0, :, pl.ds(i_old + 128 * v, 128)] for v in range(4)]
            low = [-x for x in bound]
            sums = [jnp.zeros((8, 128), jnp.float32) for _ in range(4)]
            for c in range(chunks):
                y0 = pltpu.matmul_pop(accs0[c])
                y1 = pltpu.matmul_pop(accs1[c])
                x = lhs_ref[0, pl.ds(j_now + c * CHUNK, CHUNK), :]
                x = jnp.concatenate([x, x], 1)
                load = 0 if c == 0 else None
                pltpu.matmul_acc_lhs(accs0[c], x, load_staged_rhs=load)
                pltpu.matmul_acc_lhs(accs1[c], x, load_staged_rhs=load)
                for g in range(CHUNK // 8):
                    lo, hi = 8 * g, 8 * g + 8
                    y = [y0[lo:hi, :128], y0[lo:hi, 128:], y1[lo:hi, :128], y1[lo:hi, 128:]]
                    q = [jnp.minimum(jnp.maximum(y[v], low[v]), bound[v]) for v in range(4)]
                    sb = sb_ref[0, pl.ds(j_old + c * CHUNK + lo, 8), :]
                    sums = [sums[v] + q[v] * sb for v in range(4)]
                    rows = pl.ds(r_old + c * CHUNK + lo, 8)
                    racc_ref[0, rows, :] += (q[0] + q[1]) + (q[2] + q[3])
            for v in range(4):
                cacc_ref[0, :, pl.ds(i_old + 128 * v, 128)] += sums[v]
            return carry

        lax.fori_loop(0, tasks + 1, trip, 0)
        for c in range(chunks):
            pltpu.matmul_pop(accs0[c])
            pltpu.matmul_pop(accs1[c])

    specs = [tuple(pltpu.ACC(q)((CHUNK, 256), jnp.float32) for _ in range(chunks)) for q in range(2)]
    pl.run_scoped(body, *specs)


def pair_sums(it, jt, rt, lhs, rhs, sb, b):
    days, rows, _ = lhs.shape
    own = rhs.shape[2]
    tasks = it.shape[0]
    block = lambda *shape: pl.BlockSpec((1,) + shape, lambda d, *_: (d,) + (0,) * len(shape))
    return pl.pallas_call(
        functools.partial(pair_kernel, tasks, BLK // CHUNK),
        grid_spec=pltpu.PrefetchScalarGridSpec(
            num_scalar_prefetch=3,
            grid=(days,),
            in_specs=[block(rows, 128), block(256, own), block(rows, 128), block(8, own)],
            out_specs=[block(rows + BLK, 128), block(8, own)],
        ),
        out_shape=[
            jax.ShapeDtypeStruct((days, rows + BLK, 128), jnp.float32),
            jax.ShapeDtypeStruct((days, 8, own), jnp.float32),
        ],
        compiler_params=pltpu.CompilerParams(vmem_limit_bytes=60 * 1024 * 1024),
        cost_estimate=pl.CostEstimate(
            flops=2 * days * tasks * BLK * BLK * 256, bytes_accessed=days * rows * 128 * 10, transcendentals=0
        ),
    )(it, jt, rt, lhs, rhs, sb, b)


def per_device(shards, returns, signal, earlier):
    day_dev, own = returns.shape
    me = lax.axis_index("asset")
    half = shards // 2
    extended = history(returns, earlier)
    ext, sig = [extended], [signal]
    for s in range(1, half + 1):
        perm = [((p + s) % shards, p) for p in range(shards)]
        ext.append(lax.ppermute(extended, "asset", perm))
        sig.append(lax.ppermute(signal, "asset", perm))
    ext = jnp.concatenate(ext, 1).astype(jnp.float32)
    sig = jnp.concatenate(sig, 1).astype(jnp.float32)
    span = ext.shape[0]
    ext = jnp.pad(ext, ((0, SEG - span), (0, 0)))
    k = lax.broadcasted_iota(jnp.int32, (day_dev, SEG, 1), 1)
    d = lax.broadcasted_iota(jnp.int32, (day_dev, SEG, 1), 0)
    mask = ((k >= d) & (k < d + WIN)).astype(jnp.float32)
    win = ext[None] * mask
    mean = jnp.sum(win, 1, keepdims=True) / WIN
    spread = jnp.sum(win * win, 1, keepdims=True) / WIN - mean * mean
    scale = jnp.sqrt(jnp.maximum(spread, VAR_FLOOR))
    z = (win - mean) * mask / (scale * (WIN**0.5))
    zh = lax.reduce_precision(z, 8, 7)
    zl = z - zh
    lhs = jnp.concatenate([zh, zl], 1).astype(jnp.bfloat16).transpose(0, 2, 1)
    a = sig[:, :own]
    a = jnp.where(jnp.abs(a) < TINY, TINY, a)
    u = z[:, :, :own] * a[:, None, :]
    uh = lax.reduce_precision(u, 8, 7)
    ul = u - uh
    rhs = jnp.concatenate([uh, uh, ul, ul], 1).astype(jnp.bfloat16)
    sb = jnp.broadcast_to(sig[:, :, None], sig.shape + (128,))
    b = jnp.broadcast_to((SHRINK * jnp.abs(a))[:, None, :], (day_dev, 8, own))

    blocks = own // BLK
    reach = blocks * shards // 2
    i_list = [i for i in range(blocks) for _ in range(reach)] + [0] * (blocks // 2)
    j_list = [i + x for i in range(blocks) for x in range(reach)] + [0] * (blocks // 2)
    dummy = (half + 1) * blocks
    r_list = [dummy if x == 0 else i + x for i in range(blocks) for x in range(reach)] + [0] * (blocks // 2)
    far = jnp.arange(blocks // 2, dtype=jnp.int32) + jnp.where(me >= half, blocks // 2, 0)
    body = blocks * reach
    it = jnp.array(i_list, jnp.int32).at[body:].set(far)
    jt = jnp.array(j_list, jnp.int32).at[body:].set(far + reach)
    rt = jnp.array(r_list, jnp.int32).at[body:].set(far + reach)
    racc, cacc = pair_sums(it, jt, rt, lhs, rhs, sb, b)
    row = jnp.sum(racc, 2)
    v = jnp.sum(z * sig[:, None, :], 2, keepdims=True)
    missing = []
    if half > 0 and shards > 2:
        for s in range(half + 1, shards):
            perm = [((p + s) % shards, p) for p in range(shards)]
            missing.append(perm)
    v_own = jnp.sum(z[:, :, :own] * sig[:, None, :own], 2)
    v = lax.psum(v_own, "asset")[:, :, None]
    out = jnp.sum(z[:, :, :own] * v, 1) - jnp.sum(cacc, 1) / a - row[:, :own]
    for s in range(1, half + 1):
        perm = [(p, (p + s) % shards) for p in range(shards)]
        out = out - lax.ppermute(row[:, s * own : (s + 1) * own], "asset", perm)
    return out


def solution(mesh):
    shards = mesh.shape["asset"]
    in_specs = (P("tm", "asset"), P("tm", "asset"), P(None, "asset"))
    return jax.shard_map(
        functools.partial(per_device, shards), mesh=mesh, in_specs=in_specs, out_specs=P("tm", "asset"), check_vma=False
    )
```

time: 397 us -> 190 us (0.48)
  matrix products: 320 us -> 0 us
  Pallas kernels: 0 us -> 80.5 us
  other arithmetic: 3.83 us -> 33.9 us
  blocking collectives: 44.5 us -> 28.2 us
  waiting for transfers between devices: 0 us -> 14.1 us
  local copies, waits for them, and re-layouts: 15.3 us -> 28.6 us
  loops' own time: 12.5 us -> 0 us
  starting transfers between devices: 0 us -> 4.18 us
    dot_general x4 -> x0, matrix products: 320 us -> none  [one_day(): return jnp.dot(shrunk, day_signal, preferred_element_type=jnp.float32)]
    pallas_call x0 -> x1, Pallas kernels: none -> 80.5 us  [pair_sums(): pl.pallas_call(functools.partial(pair_kernel, tasks, BLK // CHUNK), grid_...]
    all_gather x2 -> x0, blocking collectives: 19.5 us -> none  [the longest x1 14.8 us: per_device(): lax.all_gather(extended, 'asset', axis=1, tiled=True)]
    ppermute x0 -> x3, waiting for transfers between devices: none -> 14.1 us  [the longest x1 10.6 us: per_device(): ext.append(lax.ppermute(extended, 'asset', perm))]
    another operation x1 -> x0, loops' own time: 12.5 us -> none  [contribution(): return lax.map(one_day, jnp.arange(signal_cols.shape[0], dtype=jnp.int32))]
    transpose x0 -> x1, local copies, waits for them, and re-layouts: none -> 11.9 us  [per_device(): lhs = jnp.concatenate([zh, zl], 1).astype(jnp.bfloat16).transpose(0, 2, 1)]
    broadcast_in_dim x0 -> x2, local copies, waits for them, and re-layouts: none -> 11.4 us  [the longest x1 10.5 us: per_device(): sb = jnp.broadcast_to(sig[:, :, None], sig.shape + (128,))]
    reduce_sum x8 -> x4, other arithmetic: 3.25 us -> 11 us  [the longest x1 8.67 us: per_device(): row = jnp.sum(racc, 2)]
  transfers between devices with their start and end apart: 0 -> 3, of which waited for: 0 -> 2; matrix products, arithmetic and copies ran while one was open for 0% -> 3% of each run, Pallas kernels for 0% -> 0%
where the time goes in v1:
time: 190 us
  Pallas kernels  80.5 us (42%)
  other arithmetic  33.9 us (18%)
  local copies, waits for them, and re-layouts  28.6 us (15%)
  blocking collectives  28.2 us (15%)
  waiting for transfers between devices  14.1 us (7%)
  starting transfers between devices  4.18 us (2%)
    pallas_call x1, Pallas kernels, pair_sums(): pl.pallas_call(functools.partial(pair_kernel, tasks, BLK // CHUNK), grid_...  80.5 us
    all_gather x1, blocking collectives, history(): all_days = lax.all_gather(block_rows, 'tm', axis=0, tiled=True)  23.3 us
    transpose x1, local copies, waits for them, and re-layouts, per_device(): lhs = jnp.concatenate([zh, zl], 1).astype(jnp.bfloat16).transpose(0, 2, 1)  11.9 us
    ppermute x1, waiting for transfers between devices, per_device(): ext.append(lax.ppermute(extended, 'asset', perm))  10.6 us
    broadcast_in_dim x1, local copies, waits for them, and re-layouts, per_device(): sb = jnp.broadcast_to(sig[:, :, None], sig.shape + (128,))  10.5 us
    reduce_sum x1, other arithmetic, per_device(): row = jnp.sum(racc, 2)  8.67 us
    transpose x1, other arithmetic, per_device(): lhs = jnp.concatenate([zh, zl], 1).astype(jnp.bfloat16).transpose(0, 2, 1)  7.67 us
    unnamed x14, local copies, waits for them, and re-layouts  5.32 us
  transfers between devices with their start and end apart: 3, of which 2 were waited for; matrix products, arithmetic and copies ran while one was open for 3% of the time, Pallas kernels for 0%

profile of v1, /device:TPU:0, one launch (start us, length us, event | category | flops | bytes accessed | tf_op | source)
XLA Modules:
  0.0 189.6 jit_solution(1635734814860214716)
XLA Ops:
  0.0 3.0 %collective-permute-start.1 = (bf16[4,4096]{1,0:T(4,128)(2,1)}, bf16[4,4096]{1,0:T(4,128)(2,1)S(1)}, u32[]{:S(2)}, u32[]{:S(2)}) collective-permute-start(bf16[4,4096]{1,0:T(4,128)(2,1)} %param.13), channel_id=1, source_target_pairs={{1,0},{0,1},{3,2},{2,3},{5,4},{4,5},{7,6},{6,7},{9,8},{8,9},{11,10... | collective-permute-start | bytes 98312 | tf_op jit(solution)/shard_map/ppermute | solution.py:116
  3.0 23.3 %all-gather = bf16[16,4,4096]{2,1,0:T(4,128)(2,1)S(1)} all-gather(bf16[1,4,4096]{2,1,0:T(4,128)(2,1)} %bitcast.3), channel_id=1, replica_groups=mesh['tm'=16,'asset'=2] {'tm'}, dimensions={0}, use_global_device_ids=true | all-gather | bytes 557056 | tf_op jit(solution)/shard_map/all_gather | solution.py:24
  26.3 0.1 reshape.129
  26.4 1.5 fusion.9
  27.9 0.6 collective-permute-start
  28.5 0.7 copy.15
  29.2 0.7 copy.16
  29.8 0.7 copy.17
  30.5 0.1 fusion.13
  30.6 0.1 constant_dynamic-update-slice_fusion
  30.6 0.0 copy-start.2
  30.6 0.0 copy-start.3
  30.6 0.1 constant_dynamic-update-slice_fusion.2.it_ref
  30.7 0.0 copy-start.4
  30.7 0.0 collective-permute-done.1
  30.7 0.8 maximum_convert_fusion
  31.5 0.1 fusion.15
  31.6 10.6 %collective-permute-done = bf16[63,4096]{1,0:T(8,128)(2,1)S(1)} collective-permute-done((bf16[63,4096]{1,0:T(8,128)(2,1)S(1)}, bf16[63,4096]{1,0:T(8,128)(2,1)S(1)}, u32[]{:S(2)}, u32[]{:S(2)}) %collective-permute-start) | collective-permute-done | bytes 516128 | tf_op jit(solution)/shard_map/ppermute | solution.py:115
  42.2 0.1 fusion.8
  42.3 1.6 multiply_reduce_fusion
  43.9 0.1 broadcast_multiply_fusion
  44.1 4.7 %fusion.2 = (f32[4,64,8192]{2,1,0:T(8,128)S(1)}, bf16[4,64,8192]{2,1,0:T(8,128)(2,1)}, bf16[4,64,8192]{2,1,0:T(8,128)(2,1)}) fusion(f32[4,8192]{1,0:T(4,128)S(1)} %get-tuple-element.57, f32[4,8192]{1,0:T(4,128)S(1)} %get-tuple-element.56, f32[4,64]{1,0:T(4,128)S(1)} %fusion.13, f32[64,8192]{1,0:T(8,128)S(1)} %fusion.8), kind=kLoop, calls=%fused_computation.7 | loop fusion | flops 16777216 | bytes 19137536 | tf_op jit(solution)/shard_map/div | solution.py:128
  48.8 0.0 copy-done.2
  48.8 0.0 copy-done.3
  48.8 0.0 copy-done.4
  48.8 0.0 copy-start
  48.8 3.2 %copy-done = f32[4,64,8192]{2,1,0:T(8,128)} copy-done((f32[4,64,8192]{2,1,0:T(8,128)}, f32[4,64,8192]{2,1,0:T(8,128)S(1)}, u32[]{:S(2)}) %copy-start) | copy-done | bytes 8388632
  52.0 0.5 multiply_reduce_fusion.2
  52.6 4.9 %psum.7 = f32[4,64]{1,0:T(4,128)S(1)} all-reduce(f32[4,64]{1,0:T(4,128)S(1)} %multiply_reduce_fusion.2), channel_id=1, replica_groups=mesh['tm'=16,'asset'=2] {'asset'}, use_global_device_ids=true, to_apply=%region_3.4 | all-reduce | flops 256 | bytes 2048 | tf_op jit(solution)/shard_map/psum | solution.py:161
  57.5 7.7 %maximum_bitcast_fusion = bf16[4,8192,128]{1,2,0:T(8,128)(2,1)} fusion(bf16[4,64,8192]{2,1,0:T(8,128)(2,1)} %get-tuple-element.52, bf16[4,64,8192]{2,1,0:T(8,128)(2,1)} %get-tuple-element.51), kind=kLoop, calls=%fused_computation.9 | loop fusion | flops 16777216 | bytes 16777216 | tf_op jit(solution)/shard_map/transpose | solution.py:131
  65.2 11.9 %copy.8.lhs_ref = bf16[4,8192,128]{2,1,0:T(8,128)(2,1)} copy(bf16[4,8192,128]{1,2,0:T(8,128)(2,1)} %maximum_bitcast_fusion) | data formatting | bytes 16777216 | tf_op jit(solution)/shard_map/transpose | solution.py:131
  77.1 3.3 %reduce-precision_convert_fusion.1 = (bf16[4,64,4096]{2,1,0:T(8,128)(2,1)S(1)}, bf16[4,64,4096]{2,1,0:T(8,128)(2,1)S(1)}, f32[4,4096]{1,0:T(4,128)S(1)}) fusion(f32[4,64,8192]{2,1,0:T(8,128)} %copy-done, f32[4,4096]{1,0:T(4,128)S(1)} %get-tuple-element.55, f32[4,64]{1,0:T(4,128)S(1)} %psum.7), kind=kLoop, calls=%fused_computation.12 | loop fusion | flops 7323648 | bytes 8520704 | tf_op jit(solution)/shard_map/convert.2
  80.4 3.7 %pad_maximum_fusion.rhs_ref = bf16[4,256,4096]{2,1,0:T(8,128)(2,1)} fusion(bf16[4,64,4096]{2,1,0:T(8,128)(2,1)S(1)} %get-tuple-element.48, bf16[4,64,4096]{2,1,0:T(8,128)(2,1)S(1)} %get-tuple-element.47), kind=kLoop, calls=%fused_computation.10 | loop fusion | flops 33554432 | bytes 12582912 | tf_op jit(solution)/shard_map/concatenate | solution.py:137
  84.1 0.8 broadcast_in_dim.7.b_ref
  84.9 10.5 %broadcast_in_dim.6.sb_ref = f32[4,8192,128]{2,1,0:T(8,128)} broadcast(f32[4,8192]{1,0:T(4,128)S(1)} %maximum_convert_fusion), dimensions={0,1} | broadcast | bytes 16908288 | tf_op jit(solution)/shard_map/broadcast_in_dim | solution.py:138
  95.5 80.5 %shard_map.64 = (f32[4,8704,128]{2,1,0:T(8,128)}, f32[4,8,4096]{2,1,0:T(8,128)}) custom-call(s32[68]{0:T(128)} %copy-done.4, s32[68]{0:T(128)} %copy-done.2, s32[68]{0:T(128)} %copy-done.3, bf16[4,8192,128]{2,1,0:T(8,128)(2,1)} %copy.8.lhs_ref, bf16[4,256,4096]{2,1,0:T(8,128)(2,1)} %pad_maximum_fusion.rhs_ref, f32[4,8192,128]{2,1,0:T(8,128)} %broadcast_in_dim.6.sb_ref, ...), custom_call_target="tpu_custom_call" | custom-call | flops 36507222016 | bytes 41943040 | tf_op jit(solution)/shard_map/pallas_call | solution.py:88
  175.9 0.0 copy-start.1
  175.9 8.7 %reduce_sum.59 = f32[4,8704]{1,0:T(4,128)S(1)} reduce(f32[4,8704,128]{2,1,0:T(8,128)} %get-tuple-element.44, f32[]{:T(128)} %constant.93.clone.1), dimensions={2}, to_apply=%region_6.7 | reduce | flops 4421632 | bytes 17965060 | tf_op jit(solution)/shard_map/reduce_sum | solution.py:153
  184.6 0.6 collective-permute-start.2
  185.2 0.0 copy-done.1
  185.2 0.2 reduce_sum.58
  185.4 3.6 %collective-permute-done.2 = f32[4,4096]{1,0:T(4,128)S(1)} collective-permute-done((f32[4,4096]{1,0:T(4,128)S(1)}, f32[4,4096]{1,0:T(4,128)S(1)}, u32[]{:S(2)}, u32[]{:S(2)}) %collective-permute-start.2) | collective-permute-done | bytes 65568 | tf_op jit(solution)/shard_map/ppermute | solution.py:165
  189.0 0.7 fusion.10
  (2 shorter events, 0.0 us)
Async XLA Ops:
  0.0 30.7 %collective-permute-start.1 = (bf16[4,4096]{1,0:T(4,128)(2,1)}, bf16[4,4096]{1,0:T(4,128)(2,1)S(1)}, u32[]{:S(2)}, u32[]{:S(2)}) collective-permute-start(bf16[4,4096]{1,0:T(4,128)(2,1)} %param.13), channel_id=1, source_target_pairs={{1,0},{0,1},{3,2},{2,3},{5,4},{4,5},{7,6},{6,7},{9,8},{8,9},{11,10... | collective-permute-start | bytes 98312 | tf_op jit(solution)/shard_map/ppermute | solution.py:116
  27.9 14.2 %collective-permute-start = (bf16[63,4096]{1,0:T(8,128)(2,1)S(1)}, bf16[63,4096]{1,0:T(8,128)(2,1)S(1)}, u32[]{:S(2)}, u32[]{:S(2)}) collective-permute-start(bf16[63,4096]{1,0:T(8,128)(2,1)S(1)} %fusion.9), channel_id=1, source_target_pairs={{1,0},{0,1},{3,2},{2,3},{5,4},{4,5},{7,6},{6,7},{9,8},{8,9},{11,10... | collective-permute-start | bytes 1548296 | tf_op jit(solution)/shard_map/ppermute | solution.py:115
  30.6 18.2 %copy-start.2 = (s32[68]{0:T(128)}, s32[68]{0:T(128)S(1)}, u32[]{:S(2)}) copy-start(s32[68]{0:T(128)S(1)} %get-tuple-element.59.jt_ref) | copy-start | bytes 820
  30.6 18.2 %copy-start.3 = (s32[68]{0:T(128)}, s32[68]{0:T(128)S(1)}, u32[]{:S(2)}) copy-start(s32[68]{0:T(128)S(1)} %get-tuple-element.58.rt_ref) | copy-start | bytes 820
  30.7 18.1 %copy-start.4 = (s32[68]{0:T(128)}, s32[68]{0:T(128)S(1)}, u32[]{:S(2)}) copy-start(s32[68]{0:T(128)S(1)} %constant_dynamic-update-slice_fusion.2.it_ref) | copy-start | bytes 820
  48.8 3.2 %copy-start = (f32[4,64,8192]{2,1,0:T(8,128)}, f32[4,64,8192]{2,1,0:T(8,128)S(1)}, u32[]{:S(2)}) copy-start(f32[4,64,8192]{2,1,0:T(8,128)S(1)} %get-tuple-element.50) | copy-start | bytes 25165828
  175.9 9.3 %copy-start.1 = (f32[4,8,4096]{2,1,0:T(8,128)S(1)}, f32[4,8,4096]{2,1,0:T(8,128)}, u32[]{:S(2)}) copy-start(f32[4,8,4096]{2,1,0:T(8,128)} %get-tuple-element.43) | copy-start | bytes 1572868
  184.6 4.3 %collective-permute-start.2 = (f32[4,4096]{1,0:T(4,128)S(1)}, f32[4,4096]{1,0:T(4,128)S(1)}, u32[]{:S(2)}, u32[]{:S(2)}) collective-permute-start(f32[4,4096]{1,0:T(4,128)S(1)} %slice.58), channel_id=1, source_target_pairs={{0,1},{1,0},{2,3},{3,2},{4,5},{5,4},{6,7},{7,6},{8,9},{9,8},{10,11... | collective-permute-start | bytes 196616 | tf_op jit(solution)/shard_map/ppermute | solution.py:165
